TPU v7x, 32 devices: a whole 2x2x4 slice. The times are simulated.
32 devices in a mesh: seq: 8 (over y, x, core), tensor: 4 (over z).
Axes of the slice: x: 2, y: 2, z: 4, core: 2. Of those that a mesh axis runs over, the one named last changes fastest.
Arguments:
- tokens: bfloat16 [4096, 8192], P('seq', 'tensor'), may hold values from -6 to 6
- positions: int32 [4096], P('seq'), may hold values from 0 to 4095, each once
- norm_gain: float32 [8192], replicated, may hold values from 0.1 to 1.9
- w_query: bfloat16 [8192, 4096], P('seq', 'tensor'), may hold values from -0.0625 to 0.0625
- w_key: bfloat16 [8192, 1024], P('seq', 'tensor'), may hold values from -0.0625 to 0.0625
- w_value: bfloat16 [8192, 1024], P('seq', 'tensor'), may hold values from -0.0625 to 0.0625
- b_query: float32 [4096], P('tensor'), may hold values from -40 to 40
- b_key: float32 [1024], P('tensor'), may hold values from -40 to 40
- b_value: float32 [1024], P('tensor'), may hold values from -6 to 6
- w_out: bfloat16 [4096, 8192], P('tensor', 'seq'), may hold values from -0.09375 to 0.09375
Outputs:
- mixed: bfloat16 [4096, 8192], P('seq', 'tensor')
- context: bfloat16 [4096, 4096], P('seq', 'tensor')
Inputs may be any that keep to these rules, and one draw needn't show every extreme that they name: positions holds every position 0 to 4095 once.
All inputs are finite; a program needn't handle non-finite values.
Results may differ from a plain program's by a relative error of at most 0.025.
Values may be sent and summed in bfloat16 or wider, within the bound.
A program may use at most 128 MiB of HBM per device.

v0:
```python
import math
import jax
import jax.numpy as jnp
from jax import lax
from jax.sharding import PartitionSpec as P

HD = 128
NORM_EPS = 1e-06
ROPE_BASE = 1000000.0
NEG_FILL = -1e30


def rotate(values_in, positions):
    half_dim = HD // 2
    inv_freq = ROPE_BASE ** (-jnp.arange(half_dim, dtype=jnp.float32) * 2.0 / HD)
    angles = positions.astype(jnp.float32)[:, None] * inv_freq[None, :]
    cosine = jnp.cos(angles)[:, None, :]
    sines = jnp.sin(angles)[:, None, :]
    lower_half = values_in[..., :half_dim]
    upper_half = values_in[..., half_dim:]
    return jnp.concatenate(
        [lower_half * cosine - upper_half * sines, upper_half * cosine + lower_half * sines], -1
    )


def shards(tokens, positions, norm_gain, w_query, w_key, w_value, b_query, b_key, b_value, w_out):
    tok_rows = tokens.shape[0]
    features = lax.all_gather(tokens, "tensor", axis=1, tiled=True)
    inputs = features.astype(jnp.float32)
    inverse_rms = lax.rsqrt(jnp.mean(inputs * inputs, -1, keepdims=True) + NORM_EPS)
    normed = (inputs * inverse_rms * norm_gain[None, :]).astype(jnp.bfloat16)
    w_cat = jnp.concatenate((w_query, w_key, w_value), 1)
    b_cat = jnp.concatenate((b_query, b_key, b_value))
    projected = jnp.dot(
        normed, lax.all_gather(w_cat, "seq", axis=0, tiled=True), preferred_element_type=jnp.float32
    )
    projected = projected + b_cat[None, :]
    query_cols = w_query.shape[1]
    key_cols = w_key.shape[1]
    heads_here = query_cols // HD
    kv_here = key_cols // HD
    group = heads_here // kv_here
    queries = rotate(projected[:, :query_cols].reshape(tok_rows, heads_here, HD), positions).astype(
        jnp.bfloat16
    )
    queries = queries.reshape(tok_rows, kv_here, group, HD)
    keys_rot = rotate(
        projected[:, query_cols : query_cols + key_cols].reshape(tok_rows, kv_here, HD), positions
    ).astype(jnp.bfloat16)
    values = (
        projected[:, query_cols + key_cols :].astype(jnp.bfloat16).reshape(tok_rows, kv_here, HD)
    )
    scale = HD ** (-0.5)

    def attend_block(running, key_block):
        running_max, denominator, numerator = running
        block_keys, block_values, key_pos = key_block
        scores = (
            jnp.einsum("tgcd,sgd->gcts", queries, block_keys, preferred_element_type=jnp.float32)
            * scale
        )
        allowed = (key_pos[None, :] <= positions[:, None])[None, None, :, :]
        scores = jnp.where(allowed, scores, NEG_FILL)
        new_max = jnp.maximum(running_max, jnp.max(scores, -1))
        weights = jnp.where(allowed, jnp.exp(scores - new_max[..., None]), 0.0)
        rescale = jnp.exp(running_max - new_max)
        denominator = denominator * rescale + jnp.sum(weights, -1)
        numerator = numerator * rescale[..., None] + jnp.einsum(
            "gcts,sgd->gctd",
            weights.astype(jnp.bfloat16),
            block_values,
            preferred_element_type=jnp.float32,
        )
        return (new_max, denominator, numerator)

    start_state = (
        jnp.full((kv_here, group, tok_rows), NEG_FILL, jnp.float32),
        jnp.zeros((kv_here, group, tok_rows), jnp.float32),
        jnp.zeros((kv_here, group, tok_rows, HD), jnp.float32),
    )
    all_keys_in = lax.all_gather(keys_rot, "seq", axis=0, tiled=True)
    all_values_in = lax.all_gather(values, "seq", axis=0, tiled=True)
    key_pos = lax.all_gather(positions, "seq", axis=0, tiled=True)
    count = all_keys_in.shape[0]
    width = math.gcd(count, 2048)
    stacked = (
        all_keys_in.reshape(count // width, width, kv_here, HD),
        all_values_in.reshape(count // width, width, kv_here, HD),
        key_pos.reshape(count // width, width),
    )

    def stepper(carried, key_block):
        return (attend_block(carried, key_block), None)

    result, unused = lax.scan(stepper, start_state, stacked)
    unused_max, denominator, numerator = result
    per_head = numerator / denominator[..., None]
    context = (
        jnp.transpose(per_head, (2, 0, 1, 3))
        .reshape(tok_rows, heads_here * HD)
        .astype(jnp.bfloat16)
    )
    out_terms = jnp.dot(
        context,
        lax.all_gather(w_out, "seq", axis=1, tiled=True),
        preferred_element_type=jnp.float32,
    )
    summed = lax.psum_scatter(
        out_terms.astype(jnp.bfloat16), "tensor", scatter_dimension=1, tiled=True
    ).astype(jnp.float32)
    mixed = (tokens.astype(jnp.float32) + summed).astype(jnp.bfloat16)
    return (mixed, context)


def solution(mesh):
    in_specs = (
        P("seq", "tensor"),
        P("seq"),
        P(),
        P("seq", "tensor"),
        P("seq", "tensor"),
        P("seq", "tensor"),
        P("tensor"),
        P("tensor"),
        P("tensor"),
        P("tensor", "seq"),
    )
    out_specs = (P("seq", "tensor"), P("seq", "tensor"))
    return jax.shard_map(shards, mesh=mesh, in_specs=in_specs, out_specs=out_specs, check_vma=False)
```

profile of v0, /device:TPU:0, one launch (start us, length us, event | category | flops | bytes accessed | tf_op | source)
XLA Modules:
  0.0 640.7 jit_solution(5669417840117130354)
XLA Ops:
  7.2 0.0 all-gather.7.cloned.1.call-start
  7.2 0.7 all-gather.7.cloned.1.call-update
  7.9 0.0 all-gather.9.cloned.1.call-start
  8.0 3.1 pad_maximum_fusion
  11.1 0.0 all-gather.9.cloned.1.call-update
  11.2 0.0 all-gather.11.cloned.1.call-start
  11.3 1.8 multiply_cosine_fusion
  13.1 148.9 %all-gather.7.cloned.1.call-done = bf16[512,8192]{1,0:T(8,128)(2,1)} async-done(((bf16[512,2048]{1,0:T(8,128)(2,1)}), bf16[512,8192]{1,0:T(8,128)(2,1)}) %all-gather.7.cloned.1.call-update) | async-done | bytes 8388624 | tf_op jit(solution)/shard_map/all_gather | solution.py:28
  161.9 5.1 fusion.20
  167.0 120.2 %all-gather.9.cloned.1.call-done = bf16[8192,1536]{1,0:T(8,128)(2,1)} async-done(((bf16[1024,1536]{1,0:T(8,128)(2,1)}), bf16[8192,1536]{1,0:T(8,128)(2,1)}) %all-gather.9.cloned.1.call-update) | async-done | bytes 25165840 | tf_op jit(solution)/shard_map/all_gather | solution.py:35
  287.2 19.5 %fusion.27 = f32[512,1536]{1,0:T(8,128)S(1)} fusion(bf16[8192,1536]{1,0:T(8,128)(2,1)} %all-gather.9.cloned.1.call-done, bf16[512,8192]{1,0:T(8,128)(2,1)} %all-gather.7.cloned.1.call-done, f32[8192]{0:T(1024)S(1)} %copy-done.10, f32[512]{0:T(512)S(1)} %add_rsqrt_fusion, f32[1536]{0:T(1024)S(1)} %pad_maximum_fusion.3), kind=kOutput, calls=%fused_computation.35 | convolution fusion | flops 12902465536 | bytes 36741120 | tf_op jit(solution)/shard_map/dot_general | solution.py:34
  306.7 1.6 copy-done.1
  308.4 0.3 reshape.122
  308.7 0.6 fusion.32
  309.3 1.2 subtract_convert_fusion.1
  310.6 0.8 pad_maximum_fusion.2
  311.4 0.0 all-gather.13.cloned.1.call-start
  311.5 1.8 copy_bitcast_fusion
  313.3 0.0 all-gather.15.cloned.1.call-start
  313.3 0.5 all-gather.15.cloned.1.call-update
  313.9 0.0 reduce-scatter.2.cloned.1.call-start
  313.9 8.9 %all-gather = s32[8,1,512]{2,1,0:T(1,128)S(1)} all-gather(s32[1,1,512]{2,1,0:T(1,128)S(1)} %bitcast.69), channel_id=1, replica_groups=mesh['seq'=8,'tensor'=4] {'seq'}, dimensions={0}, use_global_device_ids=true | all-gather | bytes 18432 | tf_op jit(solution)/shard_map/all_gather | solution.py:83
  322.9 0.2 slice_bitcast_fusion
  323.1 0.5 copy.42
  323.5 0.3 copy-done.3
  323.8 0.8 subtract_convert_fusion
  324.7 0.1 copy.28
  324.8 0.1 copy.29
  325.0 1.5 pad_maximum_fusion.1
  326.5 12.8 %all-gather.11.cloned.1.call-done = bf16[4096,2,128]{2,0,1:T(8,128)(2,1)} async-done(((bf16[512,2,128]{2,0,1:T(8,128)(2,1)}), bf16[4096,2,128]{2,0,1:T(8,128)(2,1)}) %all-gather.11.cloned.1.call-update) | async-done | bytes 2097168 | tf_op jit(solution)/shard_map/all_gather | solution.py:81
  339.3 29.6 %all-gather.13.cloned.1.call-done = bf16[4096,2,128]{2,0,1:T(8,128)(2,1)} async-done(((bf16[512,2,128]{2,0,1:T(8,128)(2,1)}), bf16[4096,2,128]{2,0,1:T(8,128)(2,1)}) %all-gather.13.cloned.1.call-update) | async-done | bytes 2097168 | tf_op jit(solution)/shard_map/all_gather | solution.py:82
  368.9 97.0 %while.15 = (s32[]{:T(128)}, f32[2,4,512]{2,1,0:T(4,128)S(1)}, f32[2,4,512]{2,1,0:T(4,128)S(1)}, f32[2,4,512,128]{3,2,1,0:T(8,128)S(1)}, s32[2,2048]{1,0:T(2,128...) while((s32[]{:T(128)}, f32[2,4,512]{2,1,0:T(4,128)S(1)}, ...), condition=%wide.region_4.5_spmd.clone, body=%wide.region_1.4_spmd.clone.sunk | while | flops 4406661120 | bytes 112487544 | solution.py:95
  368.9 0.8 broadcast_compare_fusion.2
  369.7 16.7 %fusion.48 = (f32[2,4,512]{2,1,0:T(4,128)S(1)}, f32[2,2048,512,4]{2,1,3,0:T(8,128)}) fusion(pred[512,2048]{0,1:T(8,128)(4,1)S(1)} %broadcast_compare_fusion.2, bf16[512,2,4,128]{3,0,2,1:T(8,128)(2,1)} %get-tuple-element.222, bf16[2,2048,2,128]{3,1,0,2:T(8,128)(2,1)} %get-tuple-element.221, s32[]{:T(128)} %get-tuple-element.204), kind=kOutput, calls=%fused_computation.2.clone.1 | convolution fusion | flops 2172645376 | bytes 36717056 | tf_op jit(solution)/shard_map/while/body/eval_jaxpr/tgcd,sgd->gcts/dot_general | solution.py:59
  386.4 14.9 %fusion.49 = f32[2,4,512]{2,1,0:T(4,128)S(1)} fusion(f32[2,2048,512,4]{2,1,3,0:T(8,128)} %get-tuple-element.190, f32[2,4,512]{2,1,0:T(4,128)S(1)} %select_maximum_fusion.2, pred[512,2048]{0,1:T(8,128)(4,1)S(1)} %broadcast_compare_fusion.2), kind=kLoop, calls=%fused_computation.4.clone.1 | loop fusion | flops 41938944 | bytes 34635776 | tf_op jit(solution)/shard_map/while/body/eval_jaxpr/reduce_sum | solution.py:67
  401.3 17.8 %fusion.51 = f32[2,4,512,128]{3,2,1,0:T(8,128)S(1)} fusion(f32[2,4,512,128]{3,2,1,0:T(8,128)S(1)} %get-tuple-element.207, f32[2,2048,512,4]{2,1,3,0:T(8,128)} %get-tuple-element.190, f32[2,4,512]{2,1,0:T(4,128)S(1)} %select_maximum_fusion.2, pred[512,2048]{0,1:T(8,128)(4,1)S(1)} %broadcast_compare_fusion.2, ...), kind=kOutput, calls=%fused_computation.8.clone.1 | convolution fusion | flops 2190999552 | bytes 39879168 | tf_op jit(solution)/shard_map/while/body/eval_jaxpr/gcts,sgd->gctd/dot_general | solution.py:68
  419.2 0.8 broadcast_compare_fusion.2
  420.0 15.0 %fusion.48 = (f32[2,4,512]{2,1,0:T(4,128)S(1)}, f32[2,2048,512,4]{2,1,3,0:T(8,128)}) fusion(pred[512,2048]{0,1:T(8,128)(4,1)S(1)} %broadcast_compare_fusion.2, bf16[512,2,4,128]{3,0,2,1:T(8,128)(2,1)} %get-tuple-element.222, bf16[2,2048,2,128]{3,1,0,2:T(8,128)(2,1)} %get-tuple-element.221, s32[]{:T(128)} %get-tuple-element.204), kind=kOutput, calls=%fused_computation.2.clone.1 | convolution fusion | flops 2172645376 | bytes 36717056 | tf_op jit(solution)/shard_map/while/body/eval_jaxpr/tgcd,sgd->gcts/dot_general | solution.py:59
  435.0 15.4 %fusion.49 = f32[2,4,512]{2,1,0:T(4,128)S(1)} fusion(f32[2,2048,512,4]{2,1,3,0:T(8,128)} %get-tuple-element.190, f32[2,4,512]{2,1,0:T(4,128)S(1)} %select_maximum_fusion.2, pred[512,2048]{0,1:T(8,128)(4,1)S(1)} %broadcast_compare_fusion.2), kind=kLoop, calls=%fused_computation.4.clone.1 | loop fusion | flops 41938944 | bytes 34635776 | tf_op jit(solution)/shard_map/while/body/eval_jaxpr/reduce_sum | solution.py:67
  450.4 15.5 %fusion.51 = f32[2,4,512,128]{3,2,1,0:T(8,128)S(1)} fusion(f32[2,4,512,128]{3,2,1,0:T(8,128)S(1)} %get-tuple-element.207, f32[2,2048,512,4]{2,1,3,0:T(8,128)} %get-tuple-element.190, f32[2,4,512]{2,1,0:T(4,128)S(1)} %select_maximum_fusion.2, pred[512,2048]{0,1:T(8,128)(4,1)S(1)} %broadcast_compare_fusion.2, ...), kind=kOutput, calls=%fused_computation.8.clone.1 | convolution fusion | flops 2190999552 | bytes 39879168 | tf_op jit(solution)/shard_map/while/body/eval_jaxpr/gcts,sgd->gctd/dot_general | solution.py:68
  465.9 0.7 fusion.30
  466.6 0.8 copy.33
  467.5 0.8 convert_element_type.44
  468.2 0.0 all-gather.15.cloned.1.call-done
  468.3 17.2 %convolution_convert_fusion = bf16[512,8192]{1,0:T(8,128)(2,1)} fusion(bf16[512,1024]{1,0:T(8,128)(2,1)S(1)} %convert_element_type.44, bf16[1024,8192]{1,0:T(8,128)(2,1)} %all-gather.15.cloned.1.call-done), kind=kOutput, calls=%fused_computation.30 | convolution fusion | flops 8594128896 | bytes 26214400 | tf_op jit(solution)/shard_map/dot_general | solution.py:103
  485.4 0.0 reduce-scatter.2.cloned.1.call-update
  485.5 144.7 %reduce-scatter.2.cloned.1.call-done = bf16[512,2048]{1,0:T(8,128)(2,1)} async-done(((bf16[512,8192]{1,0:T(8,128)(2,1)}), bf16[512,2048]{1,0:T(8,128)(2,1)}) %reduce-scatter.2.cloned.1.call-update) | async-done | bytes 2097168 | tf_op jit(solution)/shard_map/reduce_scatter | solution.py:108
  630.2 3.7 add_convert_fusion
  (40 shorter events, 0.3 us)
Async XLA Ops:
  7.2 154.7 %all-gather.7.cloned.1.call-start = ((), (), s32[]{:S(2)}) async-start(), calls=%async_computation.1 | async-start | bytes 10485760 | tf_op jit(solution)/shard_map/all_gather | solution.py:28
  7.9 3.3 copy-start.6
  7.9 3.3 copy-start.7
  7.9 3.3 copy-start.8
  7.9 3.3 copy-start.9
  7.9 279.3 %all-gather.9.cloned.1.call-start = ((), (), s32[]{:S(2)}) async-start(), calls=%async_computation.2 | async-start | bytes 28311552 | tf_op jit(solution)/shard_map/all_gather | solution.py:35
  11.2 328.2 %all-gather.11.cloned.1.call-start = ((), (), s32[]{:S(2)}) async-start(), calls=%async_computation.3 | async-start | bytes 2359296 | tf_op jit(solution)/shard_map/all_gather | solution.py:81
  13.1 274.2 %copy-start.10 = (f32[8192]{0:T(1024)S(1)}, f32[8192]{0:T(1024)}, u32[]{:S(2)}) copy-start(f32[8192]{0:T(1024)} %param.14) | copy-start | bytes 98308
  306.7 1.7 copy-start.1
  309.3 13.6 %copy-start.2 = (f32[512,1536]{1,0:T(8,128)S(1)}, f32[512,1536]{1,0:T(8,128)}, u32[]{:S(2)}) copy-start(f32[512,1536]{1,0:T(8,128)} %copy-done.1) | copy-start | bytes 9437188
  311.4 57.5 %all-gather.13.cloned.1.call-start = ((), (), s32[]{:S(2)}) async-start(), calls=%async_computation.4 | async-start | bytes 2359296 | tf_op jit(solution)/shard_map/all_gather | solution.py:82
  313.3 155.0 %all-gather.15.cloned.1.call-start = ((), (), s32[]{:S(2)}) async-start(), calls=%async_computation.5 | async-start | bytes 18874368 | tf_op jit(solution)/shard_map/all_gather | solution.py:105
  313.9 316.3 %reduce-scatter.2.cloned.1.call-start = ((), (), s32[]{:S(2)}) async-start(), calls=%async_computation.6 | async-start | bytes 10485760 | tf_op jit(solution)/shard_map/reduce_scatter | solution.py:108
  322.9 1.0 copy-start.3
  324.7 44.3 %copy-start.4 = (f32[2,4,512,128]{3,2,1,0:T(8,128)S(1)}, f32[2,4,512,128]{3,2,1,0:T(8,128)}, u32[]{:S(2)}) copy-start(f32[2,4,512,128]{3,2,1,0:T(8,128)} %custom-call.2) | copy-start | bytes 6291460
  468.2 17.2 %copy-start.5 = (bf16[512,1024]{1,0:T(8,128)(2,1)}, bf16[512,1024]{1,0:T(8,128)(2,1)S(1)}, u32[]{:S(2)}) copy-start(bf16[512,1024]{1,0:T(8,128)(2,1)S(1)} %convert_element_type.44) | copy-start | bytes 3145732
  485.4 144.7 %copy-start = (bf16[512,2048]{1,0:T(8,128)(2,1)S(1)}, bf16[512,2048]{1,0:T(8,128)(2,1)}, u32[]{:S(2)}) copy-start(bf16[512,2048]{1,0:T(8,128)(2,1)} %param.12) | copy-start | bytes 6291460
Sparse Core Ops, SparseCore 0:
  9.5 152.3 all-gather.6
  163.8 123.3 all-gather.8
  311.5 27.7 all-gather.10
  341.1 27.7 all-gather.12
  370.7 89.7 all-gather.14
  485.6 144.5 reduce-scatter.1
where the time goes:
time: 641 us
  waiting for transfers between devices  457 us (71%)
  matrix products  102 us (16%)
  other arithmetic  50.8 us (8%)
  between operations  14.4 us (2%)
  blocking collectives  8.87 us (1%)
  local copies, waits for them, and re-layouts  7.19 us (1%)
    all_gather x1, waiting for transfers between devices, shards(): features = lax.all_gather(tokens, 'tensor', axis=1, tiled=True)  149 us
    reduce_scatter x1, waiting for transfers between devices, shards(): lax.psum_scatter(out_terms.astype(jnp.bfloat16), 'tensor', scatter_dimens...  145 us
    all_gather x1, waiting for transfers between devices, shards(): lax.all_gather(w_cat, 'seq', axis=0, tiled=True)  120 us
    dot_general x2, matrix products, attend_block(): jnp.einsum('gcts,sgd->gctd', weights.astype(jnp.bfloat16), block_values,...  33.3 us
    dot_general x2, matrix products, attend_block(): jnp.einsum('tgcd,sgd->gcts', queries, block_keys, preferred_element_type=...  31.7 us
    reduce_sum x2, other arithmetic, attend_block(): denominator = denominator * rescale + jnp.sum(weights, -1)  30.2 us
    all_gather x1, waiting for transfers between devices, shards(): all_values_in = lax.all_gather(values, 'seq', axis=0, tiled=True)  29.6 us
    dot_general x1, matrix products, shards(): jnp.dot(normed, lax.all_gather(w_cat, 'seq', axis=0, tiled=True), preferr...  19.5 us
  transfers between devices with their start and end apart: 6, of which 5 were waited for; matrix products, arithmetic and copies ran while one was open for 18% of the time, Pallas kernels for 0%

commit v1 on v0

--- a/solution.py
+++ b/solution.py
@@ -25,7 +25,9 @@
 
 def shards(tokens, positions, norm_gain, w_query, w_key, w_value, b_query, b_key, b_value, w_out):
     tok_rows = tokens.shape[0]
-    features = lax.all_gather(tokens, "tensor", axis=1, tiled=True)
+    features = jnp.concatenate(
+        lax.all_to_all(jnp.stack([tokens] * lax.axis_size("tensor")), "tensor", 0, 0), axis=1
+    )
     inputs = features.astype(jnp.float32)
     inverse_rms = lax.rsqrt(jnp.mean(inputs * inputs, -1, keepdims=True) + NORM_EPS)
     normed = (inputs * inverse_rms * norm_gain[None, :]).astype(jnp.bfloat16)

time: 641 us -> 576 us (0.90)
  waiting for transfers between devices: 457 us -> 370 us
  local copies, waits for them, and re-layouts: 7.19 us -> 15.2 us
  other arithmetic: 50.8 us -> 58.8 us
  starting transfers between devices: 0.24 us -> 6.65 us
    all_to_all x0 -> x1, waiting for transfers between devices: none -> 183 us  [shards(): lax.all_to_all(jnp.stack([tokens] * lax.axis_size('tensor')), 'tensor', 0...]
    all_gather x1 -> x0, waiting for transfers between devices: 149 us -> none  [shards(): features = lax.all_gather(tokens, 'tensor', axis=1, tiled=True)]
    all_gather x1, waiting for transfers between devices: 120 us -> 0.01 us  [shards(): lax.all_gather(w_cat, 'seq', axis=0, tiled=True)]
    convert_element_type x0 -> x1, other arithmetic: none -> 7.75 us  [shards(): normed = (inputs * inverse_rms * norm_gain[None, :]).astype(jnp.bfloat16)]
    all_to_all x0 -> x1, starting transfers between devices: none -> 6.49 us  [shards(): lax.all_to_all(jnp.stack([tokens] * lax.axis_size('tensor')), 'tensor', 0...]
  transfers between devices with their start and end apart: 6 -> 6, of which waited for: 5 -> 4; matrix products, arithmetic and copies ran while one was open for 18% -> 22% of each run, Pallas kernels for 0% -> 0%
where the time goes in v1:
time: 576 us; the launch traced here: 575 us
  waiting for transfers between devices  370 us (64%)
  matrix products  102 us (18%)
  other arithmetic  58.8 us (10%)
  local copies, waits for them, and re-layouts  15.2 us (3%)
  between operations  14 us (2%)
  blocking collectives  8.99 us (2%)
  starting transfers between devices  6.65 us (1%)
    all_to_all x1, waiting for transfers between devices, shards(): lax.all_to_all(jnp.stack([tokens] * lax.axis_size('tensor')), 'tensor', 0...  183 us
    reduce_scatter x1, waiting for transfers between devices, shards(): lax.psum_scatter(out_terms.astype(jnp.bfloat16), 'tensor', scatter_dimens...  145 us
    dot_general x2, matrix products, attend_block(): jnp.einsum('gcts,sgd->gctd', weights.astype(jnp.bfloat16), block_values,...  33.3 us
    dot_general x2, matrix products, attend_block(): jnp.einsum('tgcd,sgd->gcts', queries, block_keys, preferred_element_type=...  31.7 us
    reduce_sum x2, other arithmetic, attend_block(): denominator = denominator * rescale + jnp.sum(weights, -1)  30.2 us
    all_gather x1, waiting for transfers between devices, shards(): all_values_in = lax.all_gather(values, 'seq', axis=0, tiled=True)  29.7 us
    dot_general x1, matrix products, shards(): jnp.dot(normed, lax.all_gather(w_cat, 'seq', axis=0, tiled=True), preferr...  19.4 us
    dot_general x1, matrix products, shards(): jnp.dot(context, lax.all_gather(w_out, 'seq', axis=1, tiled=True), prefer...  17.2 us
  transfers between devices with their start and end apart: 6, of which 4 were waited for; matrix products, arithmetic and copies ran while one was open for 22% of the time, Pallas kernels for 0%

profile of v1, /device:TPU:0, one launch (start us, length us, event | category | flops | bytes accessed | tf_op | source)
XLA Modules:
  0.0 574.9 jit_solution(1494898244702085182)
XLA Ops:
  7.2 0.0 all-gather.6.cloned.1.call-start
  7.2 3.3 pad_maximum_fusion
  10.5 0.0 all-gather.6.cloned.1.call-update
  10.6 2.5 copy.27
  13.1 5.5 stack.2
  18.6 6.5 %all-to-all-start = ((bf16[4,512,2048]{1,2,0:T(8,128)(2,1)}), bf16[4,512,2048]{1,2,0:T(8,128)(2,1)}, u32[]{:S(2)}, u32[]{:S(2)}) async-start(bf16[4,512,2048]{1,2,0:T(8,128)(2,1)} %stack.2), calls=%async_computation | async-start | bytes 16777216 | tf_op jit(solution)/shard_map/all_to_all | solution.py:29
  25.1 1.8 multiply_cosine_fusion
  26.9 182.7 %all-to-all-done = bf16[4,512,2048]{1,2,0:T(8,128)(2,1)} async-done(((bf16[4,512,2048]{1,2,0:T(8,128)(2,1)}), bf16[4,512,2048]{1,2,0:T(8,128)(2,1)}, u32[]{:S(2)}, u32[]{:S(2)}) %all-to-all-start) | async-done | bytes 8388640 | tf_op jit(solution)/shard_map/all_to_all | solution.py:29
  209.5 5.2 multiply_reduce_fusion
  214.7 7.7 %fusion.21 = bf16[512,8192]{0,1:T(8,128)(2,1)} fusion(f32[8192]{0:T(1024)S(1)} %copy-done.8, f32[512]{0:T(512)S(1)} %add_rsqrt_fusion, bf16[4,512,2048]{1,2,0:T(8,128)(2,1)} %all-to-all-done), kind=kLoop, calls=%fused_computation.27 | loop fusion | flops 16777216 | bytes 16812032 | tf_op jit(solution)/shard_map/convert_element_type | solution.py:33
  222.5 19.4 %convolution_add_fusion = f32[512,1536]{1,0:T(8,128)S(1)} fusion(bf16[512,8192]{0,1:T(8,128)(2,1)} %fusion.21, bf16[8192,1536]{1,0:T(8,128)(2,1)} %all-gather.6.cloned.1.call-done, f32[1536]{0:T(1024)S(1)} %pad_maximum_fusion.3), kind=kOutput, calls=%fused_computation.31 | convolution fusion | flops 12885688320 | bytes 36706304 | tf_op jit(solution)/shard_map/dot_general | solution.py:36
  241.9 1.6 copy-done.2
  243.6 0.3 reshape.128
  243.9 0.6 fusion.24
  244.5 1.2 subtract_convert_fusion.1
  245.7 0.8 pad_maximum_fusion.2
  246.6 0.0 all-gather.10.cloned.1.call-start
  246.6 1.8 copy_bitcast_fusion
  248.4 0.0 all-gather.12.cloned.1.call-start
  248.5 0.5 all-gather.12.cloned.1.call-update
  249.0 0.0 reduce-scatter.2.cloned.1.call-start
  249.1 9.0 %all-gather = s32[8,1,512]{2,1,0:T(1,128)S(1)} all-gather(s32[1,1,512]{2,1,0:T(1,128)S(1)} %bitcast.78), channel_id=1, replica_groups=mesh['seq'=8,'tensor'=4] {'seq'}, dimensions={0}, use_global_device_ids=true | all-gather | bytes 18432 | tf_op jit(solution)/shard_map/all_gather | solution.py:85
  258.2 0.2 slice_bitcast_fusion
  258.3 0.5 copy.44
  258.8 0.3 copy-done.4
  259.1 0.8 subtract_convert_fusion
  259.9 0.1 copy.30
  260.1 0.1 copy.31
  260.2 1.5 pad_maximum_fusion.1
  261.8 11.9 %all-gather.8.cloned.1.call-done = bf16[4096,2,128]{2,0,1:T(8,128)(2,1)} async-done(((bf16[512,2,128]{2,0,1:T(8,128)(2,1)}), bf16[4096,2,128]{2,0,1:T(8,128)(2,1)}) %all-gather.8.cloned.1.call-update) | async-done | bytes 2097168 | tf_op jit(solution)/shard_map/all_gather | solution.py:83
  273.7 29.7 %all-gather.10.cloned.1.call-done = bf16[4096,2,128]{2,0,1:T(8,128)(2,1)} async-done(((bf16[512,2,128]{2,0,1:T(8,128)(2,1)}), bf16[4096,2,128]{2,0,1:T(8,128)(2,1)}) %all-gather.10.cloned.1.call-update) | async-done | bytes 2097168 | tf_op jit(solution)/shard_map/all_gather | solution.py:84
  303.4 97.0 %while.15 = (s32[]{:T(128)}, f32[2,4,512]{2,1,0:T(4,128)S(1)}, f32[2,4,512]{2,1,0:T(4,128)S(1)}, f32[2,4,512,128]{3,2,1,0:T(8,128)S(1)}, s32[2,2048]{1,0:T(2,128...) while((s32[]{:T(128)}, f32[2,4,512]{2,1,0:T(4,128)S(1)}, ...), condition=%wide.region_4.5_spmd.clone, body=%wide.region_1.4_spmd.clone.sunk | while | flops 4406661120 | bytes 112487544 | solution.py:97
  303.4 0.8 broadcast_compare_fusion.2
  304.2 16.7 %fusion.41 = (f32[2,4,512]{2,1,0:T(4,128)S(1)}, f32[2,2048,512,4]{2,1,3,0:T(8,128)}) fusion(pred[512,2048]{0,1:T(8,128)(4,1)S(1)} %broadcast_compare_fusion.2, bf16[512,2,4,128]{3,0,2,1:T(8,128)(2,1)} %get-tuple-element.222, bf16[2,2048,2,128]{3,1,0,2:T(8,128)(2,1)} %get-tuple-element.221, s32[]{:T(128)} %get-tuple-element.204), kind=kOutput, calls=%fused_computation.2.clone.1 | convolution fusion | flops 2172645376 | bytes 36717056 | tf_op jit(solution)/shard_map/while/body/eval_jaxpr/tgcd,sgd->gcts/dot_general | solution.py:61
  320.9 14.9 %fusion.42 = f32[2,4,512]{2,1,0:T(4,128)S(1)} fusion(f32[2,2048,512,4]{2,1,3,0:T(8,128)} %get-tuple-element.190, f32[2,4,512]{2,1,0:T(4,128)S(1)} %select_maximum_fusion.2, pred[512,2048]{0,1:T(8,128)(4,1)S(1)} %broadcast_compare_fusion.2), kind=kLoop, calls=%fused_computation.4.clone.1 | loop fusion | flops 41938944 | bytes 34635776 | tf_op jit(solution)/shard_map/while/body/eval_jaxpr/reduce_sum | solution.py:69
  335.8 17.8 %fusion.44 = f32[2,4,512,128]{3,2,1,0:T(8,128)S(1)} fusion(f32[2,4,512,128]{3,2,1,0:T(8,128)S(1)} %get-tuple-element.207, f32[2,2048,512,4]{2,1,3,0:T(8,128)} %get-tuple-element.190, f32[2,4,512]{2,1,0:T(4,128)S(1)} %select_maximum_fusion.2, pred[512,2048]{0,1:T(8,128)(4,1)S(1)} %broadcast_compare_fusion.2, ...), kind=kOutput, calls=%fused_computation.8.clone.1 | convolution fusion | flops 2190999552 | bytes 39879168 | tf_op jit(solution)/shard_map/while/body/eval_jaxpr/gcts,sgd->gctd/dot_general | solution.py:70
  353.7 0.8 broadcast_compare_fusion.2
  354.4 15.0 %fusion.41 = (f32[2,4,512]{2,1,0:T(4,128)S(1)}, f32[2,2048,512,4]{2,1,3,0:T(8,128)}) fusion(pred[512,2048]{0,1:T(8,128)(4,1)S(1)} %broadcast_compare_fusion.2, bf16[512,2,4,128]{3,0,2,1:T(8,128)(2,1)} %get-tuple-element.222, bf16[2,2048,2,128]{3,1,0,2:T(8,128)(2,1)} %get-tuple-element.221, s32[]{:T(128)} %get-tuple-element.204), kind=kOutput, calls=%fused_computation.2.clone.1 | convolution fusion | flops 2172645376 | bytes 36717056 | tf_op jit(solution)/shard_map/while/body/eval_jaxpr/tgcd,sgd->gcts/dot_general | solution.py:61
  369.5 15.4 %fusion.42 = f32[2,4,512]{2,1,0:T(4,128)S(1)} fusion(f32[2,2048,512,4]{2,1,3,0:T(8,128)} %get-tuple-element.190, f32[2,4,512]{2,1,0:T(4,128)S(1)} %select_maximum_fusion.2, pred[512,2048]{0,1:T(8,128)(4,1)S(1)} %broadcast_compare_fusion.2), kind=kLoop, calls=%fused_computation.4.clone.1 | loop fusion | flops 41938944 | bytes 34635776 | tf_op jit(solution)/shard_map/while/body/eval_jaxpr/reduce_sum | solution.py:69
  384.9 15.5 %fusion.44 = f32[2,4,512,128]{3,2,1,0:T(8,128)S(1)} fusion(f32[2,4,512,128]{3,2,1,0:T(8,128)S(1)} %get-tuple-element.207, f32[2,2048,512,4]{2,1,3,0:T(8,128)} %get-tuple-element.190, f32[2,4,512]{2,1,0:T(4,128)S(1)} %select_maximum_fusion.2, pred[512,2048]{0,1:T(8,128)(4,1)S(1)} %broadcast_compare_fusion.2, ...), kind=kOutput, calls=%fused_computation.8.clone.1 | convolution fusion | flops 2190999552 | bytes 39879168 | tf_op jit(solution)/shard_map/while/body/eval_jaxpr/gcts,sgd->gctd/dot_general | solution.py:70
  400.4 0.7 fusion.22
  401.1 0.8 copy.35
  401.9 0.8 convert_element_type.57
  402.7 0.0 all-gather.12.cloned.1.call-done
  402.7 17.2 %convolution_convert_fusion = bf16[512,8192]{1,0:T(8,128)(2,1)} fusion(bf16[512,1024]{1,0:T(8,128)(2,1)S(1)} %convert_element_type.57, bf16[1024,8192]{1,0:T(8,128)(2,1)} %all-gather.12.cloned.1.call-done), kind=kOutput, calls=%fused_computation.29 | convolution fusion | flops 8594128896 | bytes 26214400 | tf_op jit(solution)/shard_map/dot_general | solution.py:105
  419.9 0.0 reduce-scatter.2.cloned.1.call-update
  419.9 144.7 %reduce-scatter.2.cloned.1.call-done = bf16[512,2048]{1,0:T(8,128)(2,1)} async-done(((bf16[512,8192]{1,0:T(8,128)(2,1)}), bf16[512,2048]{1,0:T(8,128)(2,1)}) %reduce-scatter.2.cloned.1.call-update) | async-done | bytes 2097168 | tf_op jit(solution)/shard_map/reduce_scatter | solution.py:110
  564.6 3.7 add_convert_fusion
  (44 shorter events, 0.3 us)
Async XLA Ops:
  7.2 215.3 %all-gather.6.cloned.1.call-start = ((), (), s32[]{:S(2)}) async-start(), calls=%async_computation.2 | async-start | bytes 28311552 | tf_op jit(solution)/shard_map/all_gather | solution.py:37
  7.2 3.3 copy-start
  18.5 6.5 %copy-start.7 = (s32[512]{0:T(512)S(1)}, s32[512]{0:T(512)}, u32[]{:S(2)}) copy-start(s32[512]{0:T(512)} %param.13) | copy-start | bytes 6148
  18.5 6.5 %copy-start.9 = (f32[1024]{0:T(1024)S(1)}, f32[1024]{0:T(1024)}, u32[]{:S(2)}) copy-start(f32[1024]{0:T(1024)} %param.18) | copy-start | bytes 12292
  18.5 6.5 %copy-start.10 = (f32[256]{0:T(256)S(1)}, f32[256]{0:T(256)}, u32[]{:S(2)}) copy-start(f32[256]{0:T(256)} %param.20) | copy-start | bytes 3076
  18.6 6.5 %copy-start.11 = (f32[256]{0:T(256)S(1)}, f32[256]{0:T(256)}, u32[]{:S(2)}) copy-start(f32[256]{0:T(256)} %param.19) | copy-start | bytes 3076
  18.6 191.0 %all-to-all-start = ((bf16[4,512,2048]{1,2,0:T(8,128)(2,1)}), bf16[4,512,2048]{1,2,0:T(8,128)(2,1)}, u32[]{:S(2)}, u32[]{:S(2)}) async-start(bf16[4,512,2048]{1,2,0:T(8,128)(2,1)} %stack.2), calls=%async_computation | async-start | bytes 16777216 | tf_op jit(solution)/shard_map/all_to_all | solution.py:29
  25.0 248.6 %all-gather.8.cloned.1.call-start = ((), (), s32[]{:S(2)}) async-start(), calls=%async_computation.3 | async-start | bytes 2359296 | tf_op jit(solution)/shard_map/all_gather | solution.py:83
  26.9 187.8 %copy-start.8 = (f32[8192]{0:T(1024)S(1)}, f32[8192]{0:T(1024)}, u32[]{:S(2)}) copy-start(f32[8192]{0:T(1024)} %param.14) | copy-start | bytes 98308
  241.9 1.7 copy-start.2
  244.5 13.7 %copy-start.3 = (f32[512,1536]{1,0:T(8,128)S(1)}, f32[512,1536]{1,0:T(8,128)}, u32[]{:S(2)}) copy-start(f32[512,1536]{1,0:T(8,128)} %copy-done.2) | copy-start | bytes 9437188
  246.6 56.8 %all-gather.10.cloned.1.call-start = ((), (), s32[]{:S(2)}) async-start(), calls=%async_computation.4 | async-start | bytes 2359296 | tf_op jit(solution)/shard_map/all_gather | solution.py:84
  248.4 154.3 %all-gather.12.cloned.1.call-start = ((), (), s32[]{:S(2)}) async-start(), calls=%async_computation.5 | async-start | bytes 18874368 | tf_op jit(solution)/shard_map/all_gather | solution.py:107
  249.0 315.6 %reduce-scatter.2.cloned.1.call-start = ((), (), s32[]{:S(2)}) async-start(), calls=%async_computation.6 | async-start | bytes 10485760 | tf_op jit(solution)/shard_map/reduce_scatter | solution.py:110
  258.1 1.0 copy-start.4
  259.9 43.5 %copy-start.5 = (f32[2,4,512,128]{3,2,1,0:T(8,128)S(1)}, f32[2,4,512,128]{3,2,1,0:T(8,128)}, u32[]{:S(2)}) copy-start(f32[2,4,512,128]{3,2,1,0:T(8,128)} %custom-call.2) | copy-start | bytes 6291460
  402.7 17.2 %copy-start.6 = (bf16[512,1024]{1,0:T(8,128)(2,1)}, bf16[512,1024]{1,0:T(8,128)(2,1)S(1)}, u32[]{:S(2)}) copy-start(bf16[512,1024]{1,0:T(8,128)(2,1)S(1)} %convert_element_type.57) | copy-start | bytes 3145732
  419.9 144.7 %copy-start.1 = (bf16[512,2048]{1,0:T(8,128)(2,1)S(1)}, bf16[512,2048]{1,0:T(8,128)(2,1)}, u32[]{:S(2)}) copy-start(bf16[512,2048]{1,0:T(8,128)(2,1)} %param.12) | copy-start | bytes 6291460
Sparse Core Ops, SparseCore 0:
  10.7 127.9 all-gather.5
  246.7 26.9 all-gather.7
  275.6 27.7 all-gather.9
  305.2 89.7 all-gather.11
  420.1 144.5 reduce-scatter.1
